TPU v7x, 32 devices: a whole 2x2x4 slice. The times are simulated.
32 devices in a mesh: dp: 8 (over z, y), tensor: 4 (over x, core).
Axes of the slice: x: 2, y: 2, z: 4, core: 2. Of those that a mesh axis runs over, the one named last changes fastest.
Arguments:
- logits: bfloat16 [32, 64, 152064], P('dp', None, 'tensor'), may hold values from -3 to 3
- tokens: int32 [32, 64], P('dp'), may hold values from 0 to 152063
- lengths: int32 [32], P('dp'), may hold values from 1 to 64, 1024 in all
- group_ids: int32 [32], P('dp'), may hold values from 0 to 1, as said below
- rewards: float32 [32], P('dp'), may hold values from -4 to 4
- old_logp: float32 [32, 64], P('dp'), may hold values from -12.6 to -11.5
- ref_logp: float32 [32, 64], P('dp'), may hold values from -12.6 to -11.5
Outputs:
- token_logp: float32 [32, 64], P('dp')
- advantages: float32 [32], P('dp')
- seq_loss: float32 [32], P('dp')
- total_loss: float32 [], replicated
Inputs may be any that keep to these rules, and one draw needn't show every extreme that they name: `group_ids`: each number 0 to 1 names exactly 16 responses, placed at random over the batch. `lengths`: each response has 1 to 64 tokens, the longest exactly 64.
All inputs are finite; a program needn't handle non-finite values.
Results may differ from a plain program's by a relative error of at most 0.0003.
Values sent between devices are 32-bit elements.
A program may use at most 128 MiB of HBM per device.

v0:
```python
import jax
import jax.numpy as jnp
from jax import lax
from jax.sharding import PartitionSpec as P

GROUP = 16


CLIP_LOW = 0.2
CLIP_HIGH = 0.28
KL_WEIGHT = 0.04
STD_EPS = 0.0001


def combined_all(value, axis, join):
    pieces = jax.tree.map(lambda part: lax.all_gather(part, axis), value)
    head = jax.tree.map(lambda part: part[0], pieces)
    tail = jax.tree.map(lambda part: part[1:], pieces)
    total, _ = lax.scan(lambda total, slab: (join(total, slab), None), head, tail)
    return total


def combine_pair(former, latter):
    row_peak = jnp.maximum(former[0], latter[0])
    row_total = former[1] * jnp.exp(former[0] - row_peak) + latter[1] * jnp.exp(
        latter[0] - row_peak
    )
    return (row_peak, row_total)


def block_stats(logit_block, local_ids, vocab_width):
    values = logit_block.astype(jnp.float32)
    row_peak = jnp.max(values, axis=-1)
    row_total = jnp.sum(jnp.exp(values - row_peak[..., None]), axis=-1)
    inside = (local_ids >= 0) & (local_ids < vocab_width)
    clamped = jnp.clip(local_ids, 0, vocab_width - 1)
    picked = jnp.take_along_axis(values, clamped[..., None], axis=-1)[..., 0]
    return (row_peak, row_total, jnp.where(inside, picked, 0.0))


def local(logits, tokens, lengths, group_ids, rewards, old_logp, ref_logp):
    resp_count, seq_len, vocab_width = logits.shape
    vocab_start = lax.axis_index("tensor") * vocab_width
    local_ids = tokens - vocab_start
    positions = lax.broadcasted_iota(jnp.int32, (resp_count, seq_len), 1)
    is_valid = positions < lengths[:, None]
    row_peak, row_total, picked = block_stats(logits, local_ids, vocab_width)
    row_peak, row_total = combined_all((row_peak, row_total), "tensor", combine_pair)
    picked = lax.psum(picked, "tensor")
    token_logp = jnp.where(is_valid, picked - row_peak - jnp.log(row_total), 0.0)
    group_count = resp_count * lax.axis_size("dp") // GROUP
    group_sum, squares = lax.psum(
        (
            jax.ops.segment_sum(rewards, group_ids, num_segments=group_count),
            jax.ops.segment_sum(rewards * rewards, group_ids, num_segments=group_count),
        ),
        "dp",
    )
    group_mean = group_sum / GROUP
    spread = rewards - group_mean[group_ids]
    deviation = jnp.sqrt(jnp.maximum(squares - group_sum * group_mean, 0.0) / (GROUP - 1))
    advantages = spread / (deviation[group_ids] + STD_EPS)
    prob_ratio = jnp.exp(token_logp - old_logp)
    clipped = jnp.clip(prob_ratio, 1.0 - CLIP_LOW, 1.0 + CLIP_HIGH)
    token_gain = advantages[:, None]
    policy = -jnp.minimum(prob_ratio * token_gain, clipped * token_gain)
    ref_drift = ref_logp - token_logp
    penalty = jnp.exp(ref_drift) - ref_drift - 1.0
    token_terms = jnp.where(is_valid, policy + KL_WEIGHT * penalty, 0.0)
    seq_loss = jnp.sum(token_terms, axis=1) / lengths.astype(jnp.float32)
    total_loss = lax.psum(jnp.sum(seq_loss), "dp") / (resp_count * lax.axis_size("dp"))
    return (token_logp, advantages, seq_loss, total_loss)


def solution(mesh):
    in_specs = (
        P("dp", None, "tensor"),
        P("dp", None),
        P("dp"),
        P("dp"),
        P("dp"),
        P("dp", None),
        P("dp", None),
    )
    out_specs = (P("dp", None), P("dp"), P("dp"), P())
    return jax.shard_map(local, mesh=mesh, in_specs=in_specs, out_specs=out_specs, check_vma=False)
```

profile of v0, /device:TPU:0, one launch (start us, length us, event | category | flops | bytes accessed | tf_op | source)
XLA Modules:
  0.0 109.4 jit_solution(2576854799696201980)
XLA Ops:
  0.6 0.0 copy-start
  0.6 0.7 compare_select_fusion.1
  1.3 0.7 scatter_custom_fusion
  2.0 0.7 mul.36
  2.8 0.7 scatter_custom_fusion.1
  3.5 23.2 %all-reduce = (f32[2]{0:T(128)S(1)}, f32[2]{0:T(128)S(1)}) all-reduce(f32[2]{0:T(128)S(1)} %scatter_custom_fusion.1, f32[2]{0:T(128)S(1)} %scatter_custom_fusion), channel_id=1, replica_groups=mesh['dp'=8,'tensor'=4] {'dp'}, use_global_device_ids=true, to_apply=%region_8.9 | all-reduce | flops 4 | bytes 32 | tf_op jit(solution)/shard_map/psum | solution.py:52
  26.7 0.7 fusion.12
  27.4 0.1 reshape.64
  27.5 0.6 gather_fusion.1
  28.1 0.6 gather_fusion
  28.8 0.7 add_divide_fusion
  29.5 0.0 copy-start.4
  29.5 28.6 %fusion.18 = (f32[4,64,38016]{2,1,0:T(8,128)}, bf16[4,64]{1,0:T(4,128)(2,1)S(1)}) fusion(bf16[4,64,38016]{2,1,0:T(8,128)(2,1)} %param.9), kind=kLoop, calls=%fused_computation.45 | loop fusion | flops 19463936 | bytes 58393088 | tf_op jit(solution)/shard_map/convert_element_type | solution.py:32
  58.1 4.3 %gather_fusion.2 = f32[256]{0:T(256)S(1)} fusion(f32[4,64,38016]{2,1,0:T(8,128)} %get-tuple-element.52, s32[256]{0:T(256)S(1)} %reshape.64), kind=kCustom, calls=%fused_computation.2 | custom fusion | bytes 5120 | tf_op jit(solution)/shard_map/jit(take_along_axis)/gather | solution.py:37
  62.3 0.1 gather.13
  62.4 0.0 copy-done
  62.4 5.7 %psum.28 = f32[4,64]{1,0:T(4,128)S(1)} all-reduce(f32[4,64]{1,0:T(4,128)S(1)} %select_select_fusion), channel_id=1, replica_groups=mesh['dp'=8,'tensor'=4] {'tensor'}, use_global_device_ids=true, to_apply=%region_0.0 | all-reduce | flops 256 | bytes 2048 | tf_op jit(solution)/shard_map/psum | solution.py:49
  68.1 9.4 %exponential_reduce_fusion = f32[4,64]{1,0:T(4,128)S(1)} fusion(f32[4,64]{1,0:T(4,128)S(1)} %get-tuple-element.54, bf16[4,64,38016]{2,1,0:T(8,128)(2,1)} %param.9), kind=kLoop, calls=%fused_computation.10 | loop fusion | flops 29196032 | bytes 19466240 | tf_op jit(solution)/shard_map/reduce_sum | solution.py:34
  77.5 5.2 %all-gather.3 = f32[4,4,64]{2,1,0:T(4,128)S(1)} all-gather(f32[1,4,64]{2,1,0:T(4,128)S(1)} %bitcast.27), channel_id=3, replica_groups=mesh['dp'=8,'tensor'=4] {'tensor'}, dimensions={0}, use_global_device_ids=true | all-gather | bytes 5120 | tf_op jit(solution)/shard_map/all_gather | solution.py:16
  82.7 5.2 %all-gather.2 = f32[4,4,64]{2,1,0:T(4,128)S(1)} all-gather(f32[1,4,64]{2,1,0:T(4,128)S(1)} %get-tuple-element.55), channel_id=2, replica_groups=mesh['dp'=8,'tensor'=4] {'tensor'}, dimensions={0}, use_global_device_ids=true | all-gather | bytes 5120 | tf_op jit(solution)/shard_map/all_gather | solution.py:16
  87.9 0.1 while.12
  88.0 0.8 fusion.11
  88.8 1.1 %fusion.17 = (f32[]{:T(128)}, f32[4]{0:T(128)}) fusion(f32[4]{0:T(128)S(1)} %get-tuple-element.50, s32[4]{0:T(128)S(1)} %copy-done.1), kind=kLoop, calls=%fused_computation.44 | loop fusion | flops 11 | bytes 52 | tf_op jit(solution)/shard_map/reduce_sum | solution.py:71
  89.9 17.7 %psum.31 = f32[]{:T(128)} all-reduce(f32[]{:T(128)} %get-tuple-element.48), channel_id=1, replica_groups=mesh['dp'=8,'tensor'=4] {'dp'}, use_global_device_ids=true, to_apply=%region_11.12 | all-reduce | flops 1 | bytes 8 | tf_op jit(solution)/shard_map/psum | solution.py:71
  (22 shorter events, 0.1 us)
Async XLA Ops:
  0.6 61.8 %copy-start = (s32[4,64]{1,0:T(4,128)S(1)}, s32[4,64]{1,0:T(4,128)}, u32[]{:S(2)}) copy-start(s32[4,64]{1,0:T(4,128)} %param.10) | copy-start | bytes 3076
  29.4 58.5 %copy-start.2 = (f32[4]{0:T(128)}, f32[4]{0:T(128)S(1)}, u32[]{:S(2)}) copy-start(f32[4]{0:T(128)S(1)} %add_divide_fusion) | copy-start | bytes 52
  29.4 58.5 %copy-start.1 = (s32[4]{0:T(128)S(1)}, s32[4]{0:T(128)}, u32[]{:S(2)}) copy-start(s32[4]{0:T(128)} %param.11) | copy-start | bytes 52
  29.4 58.5 %copy-start.3 = (f32[4,64]{1,0:T(4,128)S(1)}, f32[4,64]{1,0:T(4,128)}, u32[]{:S(2)}) copy-start(f32[4,64]{1,0:T(4,128)} %param.15) | copy-start | bytes 3076
  29.5 58.5 %copy-start.4 = (f32[4,64]{1,0:T(4,128)S(1)}, f32[4,64]{1,0:T(4,128)}, u32[]{:S(2)}) copy-start(f32[4,64]{1,0:T(4,128)} %param.14) | copy-start | bytes 3076
where the time goes:
time: 110 us; the launch traced here: 109 us
  blocking collectives  56.9 us (52%)
  other arithmetic  44.2 us (40%)
  local copies, waits for them, and re-layouts  5.74 us (5%)
  between operations  2.52 us (2%)
    convert_element_type x1, other arithmetic, block_stats(): values = logit_block.astype(jnp.float32)  28.6 us
    psum x1, blocking collectives, local(): lax.psum((jax.ops.segment_sum(rewards, group_ids, num_segments=group_coun...  23.2 us
    psum x1, blocking collectives, local(): lax.psum(jnp.sum(seq_loss), 'dp') / (resp_count * lax.axis_size('dp'))  17.7 us
    all_gather x2, blocking collectives, combined_all(): pieces = jax.tree.map(lambda part: lax.all_gather(part, axis), value)  10.3 us
    reduce_sum x1, other arithmetic, block_stats(): row_total = jnp.sum(jnp.exp(values - row_peak[..., None]), axis=-1)  9.42 us
    psum x1, blocking collectives, local(): picked = lax.psum(picked, 'tensor')  5.67 us
    gather x3, local copies, waits for them, and re-layouts, block_stats(): picked = jnp.take_along_axis(values, clamped[..., None], axis=-1)[..., 0]  4.43 us

commit v1 on v0

v1 whole, which is shorter than its diff:
```python
import functools
import math

import jax
import jax.numpy as jnp
from jax import lax
from jax.experimental import pallas as pl
from jax.experimental.pallas import tpu as pltpu
from jax.sharding import PartitionSpec as P

GROUP = 16
CLIP_LOW = 0.2
CLIP_HIGH = 0.28
KL_WEIGHT = 0.04
STD_EPS = 0.0001
LOG2E = math.log2(math.e)
STRIP = 16
LANES = 128
MESH = pl.DeviceIdType.MESH


def total_wait(ref, sem):
    pltpu.make_async_copy(ref, ref, sem).wait()


def strip_stats(block, width, offset):
    tiles = width // LANES
    step = max(u for u in range(1, 13) if tiles % u == 0)

    def body(k, state):
        total, picked = state
        first = k * (step * LANES)
        base = pl.multiple_of(first, LANES)
        parts = []
        for u in range(step):
            x = block[:, pl.ds(base + u * LANES, LANES)].astype(jnp.float32)
            picked = jnp.where(offset == first + u * LANES, x, picked)
            parts.append(jnp.exp2(x * LOG2E))
        while len(parts) > 1:
            parts = [sum(parts[i : i + 2][1:], parts[i]) for i in range(0, len(parts), 2)]
        return total + parts[0], picked

    zero = jnp.zeros((STRIP, LANES), jnp.float32)
    total, picked = lax.fori_loop(0, tiles // step, body, (zero, zero))
    tail = width - tiles * LANES
    if tail:
        x = block[:, tiles * LANES :].astype(jnp.float32)
        pad = jnp.zeros((STRIP, LANES - tail), jnp.float32)
        total = total + jnp.concatenate([jnp.exp2(x * LOG2E), pad], axis=1)
        x = jnp.concatenate([x, pad], axis=1)
        picked = jnp.where(offset == tiles * LANES, x, picked)
    return total, picked


def strip_offset(tokens, resp, first, start):
    rows = lax.broadcasted_iota(jnp.int32, (STRIP, LANES), 0)
    column = jnp.zeros((STRIP, LANES), jnp.int32)
    for r in range(STRIP):
        column = jnp.where(rows == r, tokens[resp, first + r] - start, column)
    return column - lax.broadcasted_iota(jnp.int32, (STRIP, LANES), 1)


def kernel(dims, *refs):
    dp, tp, resps, seq, width = dims
    count = dp * tp
    strips = seq // STRIP
    logits, tokens, lengths, group_ids, rewards, old, ref = refs[:7]
    out_logp, out_small = refs[7:9]
    refs = refs[9:]
    blocks = refs[: resps * strips]
    acc, early, head, last, joined, send_sem, recv_sem, load_sem = refs[resps * strips :]
    d, t = lax.axis_index("dp"), lax.axis_index("tensor")
    me = d * tp + t

    loads = []
    for i in range(resps):
        for s in range(strips):
            n = i * strips + s
            loads.append(
                pltpu.make_async_copy(logits.at[i, pl.ds(s * STRIP, STRIP), :], blocks[n], load_sem.at[n])
            )
            loads[-1].start()

    barrier = pltpu.get_barrier_semaphore()

    def peer(k):
        other = lax.rem(me + k, count)
        return (other // tp, lax.rem(other, tp))

    @pl.loop(1, count)
    def _(k):
        pl.semaphore_signal(barrier, inc=1, device_id=peer(k), device_id_type=MESH)

    lane_row = lax.broadcasted_iota(jnp.int32, (resps, LANES), 0)
    zero = jnp.zeros((resps, LANES), jnp.float32)
    spread_len, spread_rew, spread_gid = zero, zero, zero
    for i in range(resps):
        hit = lane_row == i
        spread_len = jnp.where(hit, lengths[i].astype(jnp.float32), spread_len)
        spread_rew = jnp.where(hit, rewards[i], spread_rew)
        spread_gid = jnp.where(hit, group_ids[i].astype(jnp.float32), spread_gid)
    early[d, 0] = spread_len
    early[d, 1] = spread_rew
    early[d, 2] = spread_gid
    early[d, 3] = jnp.concatenate([old[...], ref[...]], axis=1)

    start = t * width
    ones = jnp.ones((8, LANES), jnp.float32)

    def send_all(buf, which):
        @pl.loop(1, count)
        def _(k):
            pltpu.make_async_remote_copy(
                buf.at[me], buf.at[me], send_sem.at[which], recv_sem.at[which], device_id=peer(k), device_id_type=MESH
            ).start()

    for i in range(resps):
        for s in range(strips):
            n = i * strips + s
            loads[n].wait()
            total, picked = strip_stats(blocks[n], width, strip_offset(tokens, i, s * STRIP, start))
            acc[pl.ds(s * STRIP, STRIP)] = total
            acc[pl.ds(seq + s * STRIP, STRIP)] = picked
        line = lax.dot_general(
            ones, acc[...], (((1,), (1,)), ((), ())),
            precision=lax.Precision.HIGHEST, preferred_element_type=jnp.float32,
        )[:1]
        if i == 0:
            pl.semaphore_wait(barrier, count - 1)

            @pl.loop(1, dp)
            def _(k):
                pltpu.make_async_remote_copy(
                    early.at[d], early.at[d], send_sem.at[0], recv_sem.at[0],
                    device_id=(lax.rem(d + k, dp), t), device_id_type=MESH,
                ).start()

        if i < resps - 1:
            head[me, i] = line
            if i == resps - 2:
                send_all(head, 1)
        else:
            last[me] = line
            send_all(last, 2)

    total_wait(early.at[pl.ds(0, dp - 1)], recv_sem.at[0])
    length = early[:, 0]
    reward = early[:, 1]
    group = early[:, 2]
    old_all = early[:, 3]
    groups = resps * dp // GROUP
    mean_of = jnp.zeros_like(reward)
    for g in range(groups):
        hit = group == float(g)
        mean = jnp.sum(jnp.where(hit, reward, 0.0), axis=(0, 1), keepdims=True) / GROUP
        mean_of = jnp.where(hit, mean, mean_of)
    spread = reward - mean_of
    dev_of = jnp.zeros_like(reward)
    for g in range(groups):
        hit = group == float(g)
        squares = jnp.sum(jnp.where(hit, spread * spread, 0.0), axis=(0, 1), keepdims=True)
        dev_of = jnp.where(hit, jnp.sqrt(squares / (GROUP - 1)), dev_of)
    advantage = spread / (dev_of + STD_EPS)

    total_wait(head.at[pl.ds(0, count - 1)], recv_sem.at[1])
    total_wait(last.at[pl.ds(0, count - 1)], recv_sem.at[2])
    for a in range(dp):
        for i in range(resps):
            parts = [head[a * tp + b, i] if i < resps - 1 else last[a * tp + b] for b in range(tp)]
            joined[a, pl.ds(i, 1)] = functools.reduce(jnp.add, parts)
    joint = joined[...]
    position = lax.broadcasted_iota(jnp.int32, joint.shape, 2).astype(jnp.float32)
    valid = (position < length) & (position < seq)
    raw = pltpu.roll(joint, LANES - seq, 2) - jnp.log(joint)
    logp = jnp.where(valid, raw, 0.0)
    ratio = jnp.exp(logp - old_all)
    clipped = jnp.clip(ratio, 1.0 - CLIP_LOW, 1.0 + CLIP_HIGH)
    policy = -jnp.minimum(ratio * advantage, clipped * advantage)
    drift = pltpu.roll(old_all, LANES - seq, 2) - logp
    penalty = jnp.exp(drift) - drift - 1.0
    terms = jnp.where(valid, policy + KL_WEIGHT * penalty, 0.0)
    seq_loss = jnp.sum(terms, axis=2, keepdims=True) / length
    total = jnp.sum(seq_loss, axis=(0, 1), keepdims=True) / (resps * dp)
    joined[...] = logp
    out_logp[...] = joined[d][:, :seq]
    out_small[2] = jnp.broadcast_to(total[0], (resps, LANES))
    joined[...] = advantage
    out_small[0] = joined[d]
    joined[...] = seq_loss
    out_small[1] = joined[d]

    total_wait(early.at[pl.ds(0, dp - 1)], send_sem.at[0])
    total_wait(head.at[pl.ds(0, count - 1)], send_sem.at[1])
    total_wait(last.at[pl.ds(0, count - 1)], send_sem.at[2])


def solution(mesh):
    dp, tp = mesh.shape["dp"], mesh.shape["tensor"]

    def local(logits, tokens, lengths, group_ids, rewards, old_logp, ref_logp):
        resps, seq, width = logits.shape
        strips = seq // STRIP
        vmem = pl.BlockSpec(memory_space=pltpu.VMEM)
        smem = pl.BlockSpec(memory_space=pltpu.SMEM)
        logp, small = pl.pallas_call(
            functools.partial(kernel, (dp, tp, resps, seq, width)),
            out_shape=(
                jax.ShapeDtypeStruct((resps, seq), jnp.float32),
                jax.ShapeDtypeStruct((3, resps, LANES), jnp.float32),
            ),
            in_specs=[pl.BlockSpec(memory_space=pl.ANY), smem, smem, smem, smem, vmem, vmem],
            out_specs=(vmem, vmem),
            scratch_shapes=[pltpu.VMEM((STRIP, width), logits.dtype)] * (resps * strips)
            + [
                pltpu.VMEM((2 * seq, LANES), jnp.float32),
                pltpu.VMEM((dp, 4, resps, LANES), jnp.float32),
                pltpu.VMEM((dp * tp, resps - 1, 1, LANES), jnp.float32),
                pltpu.VMEM((dp * tp, 1, LANES), jnp.float32),
                pltpu.VMEM((dp, resps, LANES), jnp.float32),
                pltpu.SemaphoreType.DMA((3,)),
                pltpu.SemaphoreType.DMA((3,)),
                pltpu.SemaphoreType.DMA((resps * strips,)),
            ],
            compiler_params=pltpu.CompilerParams(
                collective_id=0, has_side_effects=True, vmem_limit_bytes=48 * 1024 * 1024
            ),
        )(logits, tokens, lengths, group_ids, rewards, old_logp, ref_logp)
        return logp, small[0, :, 0], small[1, :, 0], small[2, 0, 0]

    in_specs = (
        P("dp", None, "tensor"),
        P("dp", None),
        P("dp"),
        P("dp"),
        P("dp"),
        P("dp", None),
        P("dp", None),
    )
    out_specs = (P("dp", None), P("dp"), P("dp"), P())
    return jax.shard_map(local, mesh=mesh, in_specs=in_specs, out_specs=out_specs, check_vma=False)
```

time: 110 us -> 31.6 us (0.29)
  blocking collectives: 56.9 us -> 0 us
  other arithmetic: 44.2 us -> 0 us
  Pallas kernels: 0 us -> 25 us
  between operations: 2.52 us -> 0.66 us
    psum x3 -> x0, blocking collectives: 46.6 us -> none  [the longest x1 23.2 us: local(): lax.psum((jax.ops.segment_sum(rewards, group_ids, num_segments=group_coun...]
    convert_element_type x1 -> x0, other arithmetic: 28.6 us -> none  [block_stats(): values = logit_block.astype(jnp.float32)]
    pallas_call x0 -> x1, Pallas kernels: none -> 25 us  [local(): pl.pallas_call(functools.partial(kernel, (dp, tp, resps, seq, width)), ou...]
    reduce_sum x3 -> x0, other arithmetic: 11.3 us -> none  [the longest x1 9.42 us: block_stats(): row_total = jnp.sum(jnp.exp(values - row_peak[..., None]), axis=-1)]
    all_gather x2 -> x0, blocking collectives: 10.3 us -> none  [combined_all(): pieces = jax.tree.map(lambda part: lax.all_gather(part, axis), value)]
    gather x5 -> x0, local copies, waits for them, and re-layouts: 5.71 us -> none  [the longest x3 4.43 us: block_stats(): picked = jnp.take_along_axis(values, clamped[..., None], axis=-1)[..., 0]]
    unnamed x12 -> x13, local copies, waits for them, and re-layouts: 0.03 us -> 4.58 us
    scatter-add x2 -> x0, other arithmetic: 1.43 us -> none  [the longest x1 0.72 us: local(): jax.ops.segment_sum(rewards, group_ids, num_segments=group_count)]
where the time goes in v1:
time: 31.6 us; the launch traced here: 31.4 us
  Pallas kernels  25 us (79%)
  local copies, waits for them, and re-layouts  5.75 us (18%)
  between operations  0.66 us (2%)
    pallas_call x1, Pallas kernels, local(): pl.pallas_call(functools.partial(kernel, (dp, tp, resps, seq, width)), ou...  25 us
    unnamed x13, local copies, waits for them, and re-layouts  4.58 us
    slice x2, local copies, waits for them, and re-layouts, local(): return (logp, small[0, :, 0], small[1, :, 0], small[2, 0, 0])  1.17 us

profile of v1, /device:TPU:0, one launch (start us, length us, event | category | flops | bytes accessed | tf_op | source)
XLA Modules:
  0.0 31.4 jit_solution(14556480629657860945)
XLA Ops:
  0.6 0.0 copy-start
  0.6 0.7 %copy-done = s32[4,64]{1,0:T(4,128)S(1)} copy-done((s32[4,64]{1,0:T(4,128)S(1)}, s32[4,64]{1,0:T(4,128)}, u32[]{:S(2)}) %copy-start) | copy-done | bytes 1048
  1.3 0.0 copy-start.1
  1.3 0.7 %copy-done.1 = f32[4,64]{1,0:T(4,128)S(1)} copy-done((f32[4,64]{1,0:T(4,128)S(1)}, f32[4,64]{1,0:T(4,128)}, u32[]{:S(2)}) %copy-start.1) | copy-done | bytes 1048
  2.0 0.0 copy-start.2
  2.0 0.7 %copy-done.2 = f32[4,64]{1,0:T(4,128)S(1)} copy-done((f32[4,64]{1,0:T(4,128)S(1)}, f32[4,64]{1,0:T(4,128)}, u32[]{:S(2)}) %copy-start.2) | copy-done | bytes 1048
  2.7 0.0 copy-start.3
  2.7 0.7 %copy-done.3 = s32[4]{0:T(128)S(1)} copy-done((s32[4]{0:T(128)S(1)}, s32[4]{0:T(128)}, u32[]{:S(2)}) %copy-start.3) | copy-done | bytes 40
  3.3 0.0 copy-start.4
  3.3 0.7 %copy-done.4 = s32[4]{0:T(128)S(1)} copy-done((s32[4]{0:T(128)S(1)}, s32[4]{0:T(128)}, u32[]{:S(2)}) %copy-start.4) | copy-done | bytes 40
  4.0 0.0 copy-start.5
  4.0 0.7 %copy-done.5 = f32[4]{0:T(128)S(1)} copy-done((f32[4]{0:T(128)S(1)}, f32[4]{0:T(128)}, u32[]{:S(2)}) %copy-start.5) | copy-done | bytes 40
  4.6 25.0 %shard_map.102 = (f32[4,64]{1,0:T(4,128)S(1)}, f32[3,4,128]{2,1,0:T(4,128)S(1)}) custom-call(bf16[4,64,38016]{2,1,0:T(8,128)(2,1)} %refs_0_.1, s32[4,64]{1,0:T(4,128)S(1)} %copy-done, s32[4]{0:T(128)S(1)} %copy-done.3, s32[4]{0:T(128)S(1)} %copy-done.4, f32[4]{0:T(128)S(1)} %copy-done.5, f32[4,64]{1,0:T(4,128)S(1)} %copy-done.1, f32[4,64]{1,0:T(4,128)S(1)} %copy-done.2), custom_call_target="tpu_custom_call" | custom-call | tf_op jit(solution)/shard_map/pallas_call | solution.py:205
  29.6 0.7 %slice_reduce_fusion = (f32[4]{0:T(128)}, f32[4]{0:T(128)}) fusion(f32[3,4,128]{2,1,0:T(4,128)S(1)} %get-tuple-element.7), kind=kLoop, calls=%fused_computation | loop fusion | bytes 64 | tf_op jit(solution)/shard_map/slice | solution.py:228
  30.3 0.5 %slice.11 = f32[1,1,1]{2,1,0:T(1,128)} slice(f32[3,4,128]{2,1,0:T(4,128)S(1)} %get-tuple-element.7), slice={[2:3], [0:1], [0:1]} | slice | bytes 8 | tf_op jit(solution)/shard_map/slice | solution.py:228
  30.8 0.6 %copy.12 = f32[4,64]{1,0:T(4,128)} copy(f32[4,64]{1,0:T(4,128)S(1)} %get-tuple-element.14) | data formatting | bytes 2048
Async XLA Ops:
  0.6 0.7 %copy-start = (s32[4,64]{1,0:T(4,128)S(1)}, s32[4,64]{1,0:T(4,128)}, u32[]{:S(2)}) copy-start(s32[4,64]{1,0:T(4,128)} %refs_1_.1) | copy-start | bytes 3076
  1.3 0.7 %copy-start.1 = (f32[4,64]{1,0:T(4,128)S(1)}, f32[4,64]{1,0:T(4,128)}, u32[]{:S(2)}) copy-start(f32[4,64]{1,0:T(4,128)} %refs_5_.1) | copy-start | bytes 3076
  2.0 0.7 %copy-start.2 = (f32[4,64]{1,0:T(4,128)S(1)}, f32[4,64]{1,0:T(4,128)}, u32[]{:S(2)}) copy-start(f32[4,64]{1,0:T(4,128)} %refs_6_.1) | copy-start | bytes 3076
  2.7 0.7 %copy-start.3 = (s32[4]{0:T(128)S(1)}, s32[4]{0:T(128)}, u32[]{:S(2)}) copy-start(s32[4]{0:T(128)} %refs_2_.1) | copy-start | bytes 52
  3.3 0.7 %copy-start.4 = (s32[4]{0:T(128)S(1)}, s32[4]{0:T(128)}, u32[]{:S(2)}) copy-start(s32[4]{0:T(128)} %refs_3_.1) | copy-start | bytes 52
  4.0 0.7 %copy-start.5 = (f32[4]{0:T(128)S(1)}, f32[4]{0:T(128)}, u32[]{:S(2)}) copy-start(f32[4]{0:T(128)} %refs_4_.1) | copy-start | bytes 52
